TPU v7x, 32 devices: a whole 2x2x4 slice. The times are simulated.
32 devices in a mesh: seq: 8 (over z, y), head: 4 (over x, core).
Axes of the slice: x: 2, y: 2, z: 4, core: 2. Of those that a mesh axis runs over, the one named last changes fastest.
Arguments:
- hidden_states: bfloat16 [8, 512, 3584], P(None, 'seq', 'head'), may hold values from -6 to 6
- boundary: int32 [8, 64], replicated, may hold values from 0 to 511, as said below
- valid: int32 [8, 64], replicated, may hold values from 0 to 1, as said below
- pairs: int32 [8, 2], replicated, may hold values from 0 to 7, as said below
- w_first: bfloat16 [3584, 4096], P('seq', 'head'), may hold values from -0.09375 to 0.09375
- b_first: float32 [4096], P('head'), may hold values from -3 to 3
- w_second: float32 [4096], P('head'), may hold values from -0.09375 to 0.09375
Outputs:
- step_reward: float32 [8, 64], replicated
- trace_score: float32 [8], replicated
- margin: float32 [8], replicated
Inputs may be any that keep to these rules, and one draw needn't show every extreme that they name: Within a trace the 64 boundary positions are distinct and increasing. In each trace the ones come first; every trace has 16 to 64 valid steps. `pairs`: the two traces of a pair differ.
All inputs are finite; a program needn't handle non-finite values.
Results may differ from a plain program's by a relative error of at most 0.0003.
Values may be sent and summed in bfloat16 or wider, within the bound.
A program may use at most 64 MiB of HBM per device.

v0:
```python
import jax
import jax.numpy as jnp
from jax import lax
from jax.sharding import PartitionSpec as P


def score_rows(rows, w_first, b_first, w_second):
    pre = jnp.dot(
        rows, lax.all_gather(w_first, "seq", axis=0, tiled=True), preferred_element_type=jnp.float32
    )
    return jnp.sum(jnp.maximum(pre + b_first, 0.0) * w_second, axis=-1)


def per_device(hidden_states, boundary, valid, pairs, w_first, b_first, w_second):
    traces, tok_dev, quarter = hidden_states.shape
    offset = lax.axis_index("seq") * tok_dev
    positions = offset + jnp.arange(tok_dev, dtype=jnp.int32)
    hits = boundary[:, :, None] == positions[None, None, :]
    whole = lax.all_gather(hidden_states, "head", axis=2, tiled=True)
    token_logit = score_rows(
        whole.reshape(traces * tok_dev, whole.shape[2]), w_first, b_first, w_second
    )
    token_logit = token_logit.reshape(traces, tok_dev)
    partial_logit = jnp.sum(jnp.where(hits, token_logit[:, None, :], 0.0), axis=2)
    logit = lax.psum(partial_logit, ("seq", "head"))
    live = valid == 1
    step_reward = jnp.where(live, logit, jnp.float32(0.0))
    trace_score = jnp.min(jnp.where(live, logit, jnp.float32(1e30)), axis=1)
    trace_ids = jnp.arange(traces, dtype=jnp.int32)[None, :]
    winner = jnp.sum(jnp.where(pairs[:, 0:1] == trace_ids, trace_score[None, :], 0.0), axis=1)
    loser = jnp.sum(jnp.where(pairs[:, 1:2] == trace_ids, trace_score[None, :], 0.0), axis=1)
    return (step_reward, trace_score, winner - loser)


def solution(mesh):
    placed = (P(None, "seq", "head"), P(), P(), P(), P("seq", "head"), P("head"), P("head"))
    return jax.shard_map(
        per_device, mesh=mesh, in_specs=placed, out_specs=(P(), P(), P()), check_vma=False
    )
```

profile of v0, /device:TPU:0, one launch (start us, length us, event | category | flops | bytes accessed | tf_op | source)
XLA Modules:
  0.0 212.7 jit_solution(10916989333486681788)
XLA Ops:
  7.2 0.0 all-gather.3.cloned.1.call-start
  7.2 0.7 all-gather.3.cloned.1.call-update
  7.9 0.0 all-gather.5.cloned.1.call-start
  7.9 0.7 all-gather.5.cloned.1.call-update
  8.7 0.8 slice_bitcast_fusion.1
  9.4 34.3 %all-gather.3.cloned.1.call-done = bf16[8,64,3584]{2,1,0:T(8,128)(2,1)} async-done(((bf16[8,64,896]{2,1,0:T(8,128)(2,1)}), bf16[8,64,3584]{2,1,0:T(8,128)(2,1)}) %all-gather.3.cloned.1.call-update) | async-done | bytes 3670032 | tf_op jit(solution)/shard_map/all_gather | solution.py:19
  43.8 113.7 %all-gather.5.cloned.1.call-done = bf16[3584,1024]{1,0:T(8,128)(2,1)} async-done(((bf16[448,1024]{1,0:T(8,128)(2,1)}), bf16[3584,1024]{1,0:T(8,128)(2,1)}) %all-gather.5.cloned.1.call-update) | async-done | bytes 7340048 | tf_op jit(solution)/shard_map/all_gather | solution.py:9
  157.5 0.0 copy-start
  157.5 0.0 copy-start.1
  157.5 8.2 %multiply_reduce_fusion = f32[512]{0:T(512)S(1)} fusion(bf16[512,3584]{1,0:T(8,128)(2,1)} %bitcast.7, bf16[3584,1024]{1,0:T(8,128)(2,1)} %all-gather.5.cloned.1.call-done, f32[1024]{0:T(1024)} %param.13, f32[1024]{0:T(1024)} %param.12), kind=kOutput, calls=%fused_computation | convolution fusion | flops 3760193024 | bytes 11020288 | tf_op jit(solution)/shard_map/dot_general | solution.py:8
  165.7 0.1 broadcast_in_dim.44
  165.7 0.0 copy-done
  165.7 0.3 select_reduce_fusion
  166.0 38.4 %psum.7 = f32[8,64]{1,0:T(8,128)S(1)} all-reduce(f32[8,64]{1,0:T(8,128)S(1)} %select_reduce_fusion), channel_id=1, replica_groups=mesh['seq'=8,'head'=4] {'seq','head'}, use_global_device_ids=true, to_apply=%region_2.3 | all-reduce | flops 512 | bytes 4096 | tf_op jit(solution)/shard_map/psum | solution.py:25
  204.4 0.0 copy-done.1
  204.4 0.1 select_reduce_fusion.3
  204.5 0.0 copy-start.2
  204.5 0.6 broadcast_select_fusion
  205.1 0.2 select_reduce_fusion.1
  205.4 0.5 sub.3
  205.9 0.0 copy-done.2
  (1 shorter events, 0.0 us)
Async XLA Ops:
  7.2 36.6 %all-gather.3.cloned.1.call-start = ((), (), s32[]{:S(2)}) async-start(), calls=%async_computation | async-start | bytes 4587520 | tf_op jit(solution)/shard_map/all_gather | solution.py:19
  7.9 149.6 %all-gather.5.cloned.1.call-start = ((), (), s32[]{:S(2)}) async-start(), calls=%async_computation.1 | async-start | bytes 8257536 | tf_op jit(solution)/shard_map/all_gather | solution.py:9
  157.5 8.3 %copy-start = (s32[8,64]{1,0:T(8,128)S(1)}, s32[8,64]{1,0:T(8,128)}, u32[]{:S(2)}) copy-start(s32[8,64]{1,0:T(8,128)} %param.8) | copy-start | bytes 6148
  157.5 47.0 %copy-start.1 = (s32[8,64]{1,0:T(8,128)S(1)}, s32[8,64]{1,0:T(8,128)}, u32[]{:S(2)}) copy-start(s32[8,64]{1,0:T(8,128)} %param.9) | copy-start | bytes 6148
  204.5 1.3 copy-start.2
Sparse Core Ops, SparseCore 0:
  9.5 34.1 all-gather.2
  45.9 111.4 all-gather.4
where the time goes:
time: 213 us
  waiting for transfers between devices  149 us (70%)
  blocking collectives  38.4 us (18%)
  between operations  14.1 us (7%)
  matrix products  8.19 us (4%)
    all_gather x1, waiting for transfers between devices, score_rows(): lax.all_gather(w_first, 'seq', axis=0, tiled=True)  114 us
    psum x1, blocking collectives, per_device(): logit = lax.psum(partial_logit, ('seq', 'head'))  38.4 us
    all_gather x1, waiting for transfers between devices, per_device(): whole = lax.all_gather(hidden_states, 'head', axis=2, tiled=True)  34.3 us
    dot_general x1, matrix products, score_rows(): jnp.dot(rows, lax.all_gather(w_first, 'seq', axis=0, tiled=True), preferr...  8.19 us
  transfers between devices with their start and end apart: 2, of which 2 were waited for; matrix products, arithmetic and copies ran while one was open for 0% of the time, Pallas kernels for 0%

commit v1 on v0

--- a/solution.py
+++ b/solution.py
@@ -1,7 +1,13 @@
+import functools
+
 import jax
 import jax.numpy as jnp
 from jax import lax
+from jax.experimental import pallas as pl
+from jax.experimental.pallas import tpu as pltpu
 from jax.sharding import PartitionSpec as P
+
+MESH = pl.DeviceIdType.MESH
 
 
 def score_rows(rows, w_first, b_first, w_second):
@@ -32,8 +38,282 @@
     return (step_reward, trace_score, winner - loser)
 
 
+def kernel(
+    n_seq, n_head, hid, bnd, valid, pairs, w, b, w2, reward, score, margin,
+    xout, xin, xacc, xup, xdn, xall, wown, wall, psend, precv, fsend, frecv,
+    s_x1, r_x1, s_w, r_w, s_x2, r_up, r_dn, s_x3, r_x3, s_p, r_p, s_f, r_f,
+):
+    traces, toks, _ = hid.shape
+    half = traces // 2
+    planes = n_seq // 2
+    depth = w.shape[0]
+    cols = w.shape[1] // 2
+    s = lax.axis_index("seq")
+    h = lax.axis_index("head")
+    z = s // 2
+    y = s % 2
+    other = 1 - y
+
+    def remote(src, dst, send, recv, to_s, to_h):
+        return pltpu.make_async_remote_copy(
+            src_ref=src, dst_ref=dst, send_sem=send, recv_sem=recv,
+            device_id=(to_s, to_h), device_id_type=MESH,
+        )
+
+    across = s + 1 - 2 * y
+    h_core = h + 1 - 2 * (h % 2)
+    h_x = lax.rem(h + 2, n_head)
+
+    def pick(t):
+        pos = lax.broadcasted_iota(jnp.int32, (toks, bnd.shape[1]), 0) + s * toks
+        hot = jnp.where(bnd[pl.ds(t, 1), :] == pos, 1.0, 0.0).astype(jnp.bfloat16)
+        got = lax.dot_general(
+            hot, hid[t], (((0,), (0,)), ((), ())), preferred_element_type=jnp.float32
+        )
+        return got.astype(jnp.bfloat16)
+
+    def copy_x1(k):
+        return remote(xout.at[k], xin.at[k], s_x1.at[k], r_x1.at[k], across, h)
+
+    for k in range(half):
+        xout[k] = pick(other * half + k)
+        copy_x1(k).start()
+
+    def my_cols(which):
+        return pl.ds(pl.multiple_of(which * cols, cols), cols)
+
+    rows = pl.ds(pl.multiple_of(y * depth, depth), depth)
+    wown[...] = w[:, my_cols(other)]
+    copy_w = remote(wown, wall.at[rows], s_w, r_w, across, h)
+    copy_w.start()
+    wall[rows, :] = w[:, my_cols(y)]
+
+    for k in range(half):
+        xacc[k] = pick(y * half + k)
+
+    is_root = z == h
+    from_up = (z >= h) & (z < planes - 1)
+    from_dn = (z <= h) & (z > 0)
+
+    def copy_down(k):
+        return remote(xacc.at[k], xup.at[k], s_x2.at[k], r_up.at[k], lax.rem(s + n_seq - 2, n_seq), h)
+
+    def copy_up(k):
+        return remote(xacc.at[k], xdn.at[k], s_x2.at[k], r_dn.at[k], lax.rem(s + 2, n_seq), h)
+
+    def chain(k):
+        copy_x1(k).wait_recv()
+        xacc[k] = xacc[k] + xin[k]
+
+        @pl.when(from_up)
+        def _():
+            copy_down(k).wait_recv()
+            xacc[k] = xacc[k] + xup[k]
+
+        @pl.when(from_dn)
+        def _():
+            copy_up(k).wait_recv()
+            xacc[k] = xacc[k] + xdn[k]
+
+        @pl.when(z > h)
+        def _():
+            copy_down(k).start()
+
+        @pl.when(z < h)
+        def _():
+            copy_up(k).start()
+
+        @pl.when(is_root)
+        def _():
+            xall[y * half + k] = xacc[k]
+
+    same_core = (h % 2) == (z % 2)
+    same_x = (h // 2) == (z // 2)
+
+    def copy_x3(t, way):
+        to_s, to_h = ((s, h_core), (across, h), (s, h_x))[way]
+        return remote(xall.at[t], xall.at[t], s_x3.at[t, way], r_x3.at[t], to_s, to_h)
+
+    def spread(k):
+        for y0 in range(2):
+            t = y0 * half + k
+
+            @pl.when(jnp.logical_not(is_root & (y == y0)))
+            def _():
+                copy_x3(t, 0).wait_recv()
+
+            @pl.when(same_core & same_x & (y == y0))
+            def _():
+                copy_x3(t, 2).start()
+
+            @pl.when(same_core & (y == y0))
+            def _():
+                copy_x3(t, 1).start()
+
+            @pl.when(same_core)
+            def _():
+                copy_x3(t, 0).start()
+
+    for k in range(half):
+        chain(k)
+        if k >= 1:
+            spread(k - 1)
+    spread(half - 1)
+
+    copy_w.wait_recv()
+
+    def copy_p(t):
+        to_s = lax.rem(s + n_seq - 2, n_seq) if t < half else lax.rem(s + 2, n_seq)
+        return remote(psend.at[t], precv.at[t], s_p.at[t], r_p.at[t], to_s, h)
+
+    bias = b[:, my_cols(y)]
+    out_row = w2[:, my_cols(y)]
+    lanes = lax.broadcasted_iota(jnp.int32, (xall.shape[1], 128), 1)
+    fsend[...] = jnp.zeros_like(fsend)
+    for k in range(half):
+        for t in (k, half + k):
+            first = planes - 1 if t < half else 0
+            last = 0 if t < half else planes - 1
+            psend[t] = jnp.dot(xall[t], wall[...], preferred_element_type=jnp.float32)
+
+            @pl.when(z != first)
+            def _():
+                copy_p(t).wait_recv()
+                psend[t] = psend[t] + precv[t]
+
+            @pl.when(z != last)
+            def _():
+                copy_p(t).start()
+
+            @pl.when(z == last)
+            def _():
+                act = jnp.maximum(psend[t] + bias, 0.0) * out_row
+                part = jnp.sum(act, axis=1, keepdims=True)
+                fsend[...] = fsend[...] + jnp.where(lanes == t, part, 0.0)
+
+    is_end = (z == 0) | (z == planes - 1)
+    slots = 4 * n_head
+    me = s * n_head + h
+    n_dev = n_seq * n_head
+    slot = jnp.where(z == 0, 0, 1) * (2 * n_head) + y * n_head + h
+
+    def copy_f(d):
+        to = lax.rem(me + d, n_dev)
+        return remote(
+            frecv.at[slot], frecv.at[slot], s_f.at[d], r_f.at[slot], to // n_head, lax.rem(to, n_head)
+        )
+
+    @pl.when(is_end)
+    def _():
+        frecv[slot] = jnp.transpose(fsend[...])[: frecv.shape[1], :]
+        for d in range(1, n_dev):
+            copy_f(d).start()
+
+    logit = jnp.zeros(frecv.shape[1:], jnp.float32)
+    for i in range(slots):
+
+        @pl.when(jnp.logical_not(is_end & (slot == i)))
+        def _():
+            remote(frecv.at[i], frecv.at[i], s_f.at[0], r_f.at[i], across, h).wait_recv()
+
+        logit = logit + frecv[i]
+
+    live = valid[...] == 1
+    reward[...] = jnp.where(live, logit, 0.0)
+    low = jnp.min(jnp.where(live, logit, 1e30), axis=1, keepdims=True)
+    score[...] = low
+    eye = lax.broadcasted_iota(jnp.int32, (traces, traces), 0) == lax.broadcasted_iota(
+        jnp.int32, (traces, traces), 1
+    )
+    row = jnp.sum(jnp.where(eye, low, 0.0), axis=0, keepdims=True)
+    ids = lax.broadcasted_iota(jnp.int32, (pairs.shape[0], traces), 1)
+    winner = jnp.sum(jnp.where(pairs[:, 0:1] == ids, row, 0.0), axis=1, keepdims=True)
+    loser = jnp.sum(jnp.where(pairs[:, 1:2] == ids, row, 0.0), axis=1, keepdims=True)
+    margin[...] = winner - loser
+
+    copy_w.wait_send()
+    for k in range(half):
+        copy_x1(k).wait_send()
+
+        @pl.when(jnp.logical_not(is_root))
+        def _():
+            copy_down(k).wait_send()
+
+        for y0 in range(2):
+            t = y0 * half + k
+
+            @pl.when(same_core & same_x & (y == y0))
+            def _():
+                copy_x3(t, 2).wait_send()
+
+            @pl.when(same_core & (y == y0))
+            def _():
+                copy_x3(t, 1).wait_send()
+
+            @pl.when(same_core)
+            def _():
+                copy_x3(t, 0).wait_send()
+
+            @pl.when(z != (0 if t < half else planes - 1))
+            def _():
+                copy_p(t).wait_send()
+
+    @pl.when(is_end)
+    def _():
+        for d in range(1, n_dev):
+            copy_f(d).wait_send()
+
+
+def fused(n_seq, n_head, hidden_states, boundary, valid, pairs, w_first, b_first, w_second):
+    traces, toks, feats = hidden_states.shape
+    steps = boundary.shape[1]
+    depth, width = w_first.shape
+    half, cols = traces // 2, width // 2
+    bf16, f32 = jnp.bfloat16, jnp.float32
+    dma = pltpu.SemaphoreType.DMA
+    vmem = pl.BlockSpec(memory_space=pltpu.VMEM)
+    reward, score, margin = pl.pallas_call(
+        functools.partial(kernel, n_seq, n_head),
+        out_shape=(
+            jax.ShapeDtypeStruct((traces, steps), f32),
+            jax.ShapeDtypeStruct((traces, 1), f32),
+            jax.ShapeDtypeStruct((pairs.shape[0], 1), f32),
+        ),
+        in_specs=[vmem] * 7,
+        out_specs=(vmem,) * 3,
+        scratch_shapes=[
+            pltpu.VMEM((half, steps, feats), bf16),
+            pltpu.VMEM((half, steps, feats), bf16),
+            pltpu.VMEM((half, steps, feats), bf16),
+            pltpu.VMEM((half, steps, feats), bf16),
+            pltpu.VMEM((half, steps, feats), bf16),
+            pltpu.VMEM((traces, steps, feats), bf16),
+            pltpu.VMEM((depth, cols), bf16),
+            pltpu.VMEM((2 * depth, cols), bf16),
+            pltpu.VMEM((traces, steps, cols), f32),
+            pltpu.VMEM((traces, steps, cols), f32),
+            pltpu.VMEM((steps, 128), f32),
+            pltpu.VMEM((4 * n_head, traces, steps), f32),
+            dma((half,)), dma((half,)),
+            dma, dma,
+            dma((half,)), dma((half,)), dma((half,)),
+            dma((traces, 3)), dma((traces,)),
+            dma((traces,)), dma((traces,)),
+            dma((n_seq * n_head,)), dma((4 * n_head,)),
+        ],
+        compiler_params=pltpu.CompilerParams(has_side_effects=True),
+    )(
+        hidden_states, boundary, valid, pairs, w_first,
+        b_first.reshape(1, width), w_second.reshape(1, width),
+    )
+    return reward, score.reshape(traces), margin.reshape(pairs.shape[0])
+
+
 def solution(mesh):
+    n_seq, n_head = mesh.shape["seq"], mesh.shape["head"]
+    paired = n_seq == 2 * n_head and n_head % 4 == 0
+    body = functools.partial(fused, n_seq, n_head) if paired else per_device
     placed = (P(None, "seq", "head"), P(), P(), P(), P("seq", "head"), P("head"), P("head"))
     return jax.shard_map(
-        per_device, mesh=mesh, in_specs=placed, out_specs=(P(), P(), P()), check_vma=False
-    )
+        body, mesh=mesh, in_specs=placed, out_specs=(P(), P(), P()), check_vma=False
+    )

time: 213 us -> 199 us (0.934)
  Pallas kernels: 0 us -> 195 us
  waiting for transfers between devices: 149 us -> 0 us
  blocking collectives: 38.4 us -> 0 us
  between operations: 14.1 us -> 0.67 us
  matrix products: 8.19 us -> 0 us
    pallas_call x0 -> x1, Pallas kernels: none -> 195 us  [fused(): pl.pallas_call(functools.partial(kernel, n_seq, n_head), out_shape=(jax.S...]
    all_gather x2 -> x0, waiting for transfers between devices: 148 us -> none  [the longest x1 114 us: score_rows(): lax.all_gather(w_first, 'seq', axis=0, tiled=True)]
    psum x1 -> x0, blocking collectives: 38.4 us -> none  [per_device(): logit = lax.psum(partial_logit, ('seq', 'head'))]
    dot_general x1 -> x0, matrix products: 8.19 us -> none  [score_rows(): jnp.dot(rows, lax.all_gather(w_first, 'seq', axis=0, tiled=True), preferr...]
    unnamed x6 -> x10, local copies, waits for them, and re-layouts: 0.01 us -> 2.6 us
  transfers between devices with their start and end apart: 2 -> 0, of which waited for: 2 -> 0; matrix products, arithmetic and copies ran while one was open for 0% -> 0% of each run, Pallas kernels for 0% -> 0%
where the time goes in v1:
time: 199 us
  Pallas kernels  195 us (98%)
  local copies, waits for them, and re-layouts  2.6 us (1%)
    pallas_call x1, Pallas kernels, fused(): pl.pallas_call(functools.partial(kernel, n_seq, n_head), out_shape=(jax.S...  195 us

profile of v1, /device:TPU:0, one launch (start us, length us, event | category | flops | bytes accessed | tf_op | source)
XLA Modules:
  0.0 199.3 jit_solution(4227770826307656941)
XLA Ops:
  0.6 0.0 copy-start.3
  0.6 0.7 copy-done.3
  1.3 0.7 copy.11.pairs
  2.0 194.7 %shard_map.94 = (f32[8,64]{1,0:T(8,128)}, f32[8,1]{1,0:T(8,128)}, f32[8,1]{1,0:T(8,128)}) custom-call(bf16[8,64,896]{2,1,0:T(8,128)(2,1)} %hid.1, s32[8,64]{1,0:T(8,128)} %bnd.1, s32[8,64]{1,0:T(8,128)} %valid.1, s32[8,2]{1,0:T(8,128)} %copy.11.pairs, bf16[448,1024]{1,0:T(8,128)(2,1)} %w.1, f32[1,1024]{1,0:T(1,128)} %bitcast.2, f32[1,1024]{1,0:T(1,128)} %bitcast.3), custom_call_target="tpu_custom_call" | custom-call | tf_op jit(solution)/shard_map/pallas_call | solution.py:275
  196.7 0.0 copy-start.1
  196.7 0.0 copy-start
  196.7 0.7 copy-done.1
  197.4 0.0 copy-start.2
  197.4 0.6 reduce
  198.0 0.0 copy-done
  198.0 0.6 reduce.1
  198.7 0.0 copy-done.2
  198.7 0.6 copy.13
Async XLA Ops:
  0.6 0.7 copy-start.3
  196.7 0.7 copy-start.1
  196.7 1.3 copy-start
  197.4 1.3 copy-start.2

commit v2 on v1

--- a/solution.py
+++ b/solution.py
@@ -75,21 +75,31 @@
     def copy_x1(k):
         return remote(xout.at[k], xin.at[k], s_x1.at[k], r_x1.at[k], across, h)
 
+    def my_cols(which):
+        return pl.ds(pl.multiple_of(which * cols, cols), cols)
+
+    part = depth // 2
+
+    def copy_w(i):
+        rows = pl.ds(pl.multiple_of(y * depth + i * part, part), part)
+        return remote(wown.at[pl.ds(i * part, part)], wall.at[rows], s_w.at[i], r_w.at[i], across, h)
+
+    wown[...] = w[:, my_cols(other)]
+    copy_w(0).start()
     for k in range(half):
         xout[k] = pick(other * half + k)
         copy_x1(k).start()
-
-    def my_cols(which):
-        return pl.ds(pl.multiple_of(which * cols, cols), cols)
-
-    rows = pl.ds(pl.multiple_of(y * depth, depth), depth)
-    wown[...] = w[:, my_cols(other)]
-    copy_w = remote(wown, wall.at[rows], s_w, r_w, across, h)
-    copy_w.start()
-    wall[rows, :] = w[:, my_cols(y)]
+    copy_w(1).start()
+    wall[pl.ds(pl.multiple_of(y * depth, depth), depth), :] = w[:, my_cols(y)]
 
     for k in range(half):
         xacc[k] = pick(y * half + k)
+
+    same_core = (h % 2) == (z % 2)
+
+    def copy_x3(t, way):
+        to_s, to_h = ((s, h_core), (across, h), (s, h_x))[way]
+        return remote(xall.at[t], xall.at[t], s_x3.at[t, way], r_x3.at[t], to_s, to_h)
 
     is_root = z == h
     from_up = (z >= h) & (z < planes - 1)
@@ -125,71 +135,79 @@
 
         @pl.when(is_root)
         def _():
-            xall[y * half + k] = xacc[k]
-
-    same_core = (h % 2) == (z % 2)
-    same_x = (h // 2) == (z // 2)
-
-    def copy_x3(t, way):
-        to_s, to_h = ((s, h_core), (across, h), (s, h_x))[way]
-        return remote(xall.at[t], xall.at[t], s_x3.at[t, way], r_x3.at[t], to_s, to_h)
+            t = y * half + k
+            xall[t] = xacc[k]
+            copy_x3(t, 1).start()
+            copy_x3(t, 2).start()
+            copy_x3(t, 0).start()
 
     def spread(k):
-        for y0 in range(2):
-            t = y0 * half + k
-
-            @pl.when(jnp.logical_not(is_root & (y == y0)))
-            def _():
-                copy_x3(t, 0).wait_recv()
-
-            @pl.when(same_core & same_x & (y == y0))
-            def _():
-                copy_x3(t, 2).start()
-
-            @pl.when(same_core & (y == y0))
+        t = y * half + k
+
+        @pl.when(jnp.logical_not(is_root))
+        def _():
+            copy_x3(t, 0).wait_recv()
+
+            @pl.when(same_core)
             def _():
                 copy_x3(t, 1).start()
-
-            @pl.when(same_core)
-            def _():
                 copy_x3(t, 0).start()
 
+    def spread_far(k):
+        t = other * half + k
+        copy_x3(t, 0).wait_recv()
+
+        @pl.when(same_core)
+        def _():
+            copy_x3(t, 0).start()
+
     for k in range(half):
         chain(k)
-        if k >= 1:
-            spread(k - 1)
-    spread(half - 1)
-
-    copy_w.wait_recv()
-
-    def copy_p(t):
-        to_s = lax.rem(s + n_seq - 2, n_seq) if t < half else lax.rem(s + 2, n_seq)
+    for k in range(half):
+        spread(k)
+    for k in range(half):
+        spread_far(k)
+    for i in range(2):
+        copy_w(i).wait_recv()
+
+    def copy_p(t, down):
+        to_s = lax.rem(s + n_seq - 2, n_seq) if down else lax.rem(s + 2, n_seq)
         return remote(psend.at[t], precv.at[t], s_p.at[t], r_p.at[t], to_s, h)
 
     bias = b[:, my_cols(y)]
     out_row = w2[:, my_cols(y)]
     lanes = lax.broadcasted_iota(jnp.int32, (xall.shape[1], 128), 1)
     fsend[...] = jnp.zeros_like(fsend)
-    for k in range(half):
-        for t in (k, half + k):
-            first = planes - 1 if t < half else 0
-            last = 0 if t < half else planes - 1
-            psend[t] = jnp.dot(xall[t], wall[...], preferred_element_type=jnp.float32)
-
-            @pl.when(z != first)
+
+    def reduce_step(tick, _):
+        for down in (True, False):
+            first = planes - 1 if down else 0
+            last = planes - 1 - first
+            k = tick - (planes - 1 - z if down else z)
+            t = k if down else half + k
+
+            @pl.when((k >= 0) & (k < half))
             def _():
-                copy_p(t).wait_recv()
-                psend[t] = psend[t] + precv[t]
-
-            @pl.when(z != last)
-            def _():
-                copy_p(t).start()
-
-            @pl.when(z == last)
-            def _():
-                act = jnp.maximum(psend[t] + bias, 0.0) * out_row
-                part = jnp.sum(act, axis=1, keepdims=True)
-                fsend[...] = fsend[...] + jnp.where(lanes == t, part, 0.0)
+                psend[t] = jnp.dot(xall[t], wall[...], preferred_element_type=jnp.float32)
+
+                @pl.when(z != first)
+                def _():
+                    copy_p(t, down).wait_recv()
+                    psend[t] = psend[t] + precv[t]
+
+                @pl.when(z != last)
+                def _():
+                    copy_p(t, down).start()
+
+                @pl.when(z == last)
+                def _():
+                    act = jnp.maximum(psend[t] + bias, 0.0) * out_row
+                    total = jnp.sum(act, axis=1, keepdims=True)
+                    fsend[...] = fsend[...] + jnp.where(lanes == t, total, 0.0)
+
+        return 0
+
+    lax.fori_loop(0, half + planes - 1, reduce_step, 0)
 
     is_end = (z == 0) | (z == planes - 1)
     slots = 4 * n_head
@@ -231,7 +249,8 @@
     loser = jnp.sum(jnp.where(pairs[:, 1:2] == ids, row, 0.0), axis=1, keepdims=True)
     margin[...] = winner - loser
 
-    copy_w.wait_send()
+    for i in range(2):
+        copy_w(i).wait_send()
     for k in range(half):
         copy_x1(k).wait_send()
 
@@ -239,24 +258,25 @@
         def _():
             copy_down(k).wait_send()
 
-        for y0 in range(2):
-            t = y0 * half + k
-
-            @pl.when(same_core & same_x & (y == y0))
-            def _():
-                copy_x3(t, 2).wait_send()
-
-            @pl.when(same_core & (y == y0))
-            def _():
-                copy_x3(t, 1).wait_send()
+        for t, near in ((y * half + k, True), (other * half + k, False)):
 
             @pl.when(same_core)
             def _():
                 copy_x3(t, 0).wait_send()
-
-            @pl.when(z != (0 if t < half else planes - 1))
-            def _():
-                copy_p(t).wait_send()
+                if near:
+                    copy_x3(t, 1).wait_send()
+
+        @pl.when(is_root)
+        def _():
+            copy_x3(y * half + k, 2).wait_send()
+
+        @pl.when(z != 0)
+        def _():
+            copy_p(k, True).wait_send()
+
+        @pl.when(z != planes - 1)
+        def _():
+            copy_p(half + k, False).wait_send()
 
     @pl.when(is_end)
     def _():
@@ -295,7 +315,7 @@
             pltpu.VMEM((steps, 128), f32),
             pltpu.VMEM((4 * n_head, traces, steps), f32),
             dma((half,)), dma((half,)),
-            dma, dma,
+            dma((2,)), dma((2,)),
             dma((half,)), dma((half,)), dma((half,)),
             dma((traces, 3)), dma((traces,)),
             dma((traces,)), dma((traces,)),

time: 199 us -> 83.2 us (0.42)
  Pallas kernels: 195 us -> 78.5 us
    pallas_call x1, Pallas kernels: 195 us -> 78.5 us  [fused(): pl.pallas_call(functools.partial(kernel, n_seq, n_head), out_shape=(jax.S...]
where the time goes in v2:
time: 83.2 us; the launch traced here: 83 us
  Pallas kernels  78.5 us (94%)
  local copies, waits for them, and re-layouts  2.6 us (3%)
  other arithmetic  1.25 us (2%)
    pallas_call x1, Pallas kernels, fused(): pl.pallas_call(functools.partial(kernel, n_seq, n_head), out_shape=(jax.S...  78.5 us
    unnamed x10, local copies, waits for them, and re-layouts  2.6 us

profile of v2, /device:TPU:0, one launch (start us, length us, event | category | flops | bytes accessed | tf_op | source)
XLA Modules:
  0.0 83.0 jit_solution(15487752513230546611)
XLA Ops:
  0.6 0.0 copy-start.3
  0.6 0.7 copy-done.3
  1.3 0.7 copy.11.pairs
  2.0 78.5 %shard_map.94 = (f32[8,64]{1,0:T(8,128)}, f32[8,1]{1,0:T(8,128)}, f32[8,1]{1,0:T(8,128)}) custom-call(bf16[8,64,896]{2,1,0:T(8,128)(2,1)} %hid.1, s32[8,64]{1,0:T(8,128)} %bnd.1, s32[8,64]{1,0:T(8,128)} %valid.1, s32[8,2]{1,0:T(8,128)} %copy.11.pairs, bf16[448,1024]{1,0:T(8,128)(2,1)} %w.1, f32[1,1024]{1,0:T(1,128)} %bitcast.2, f32[1,1024]{1,0:T(1,128)} %bitcast.3), custom_call_target="tpu_custom_call" | custom-call | tf_op jit(solution)/shard_map/pallas_call | solution.py:295
  80.5 0.0 copy-start.1
  80.5 0.0 copy-start
  80.5 0.7 copy-done.1
  81.1 0.0 copy-start.2
  81.1 0.6 reduce
  81.8 0.0 copy-done
  81.8 0.6 reduce.1
  82.4 0.0 copy-done.2
  82.4 0.6 copy.13
Async XLA Ops:
  0.6 0.7 copy-start.3
  80.5 0.7 copy-start.1
  80.5 1.3 %copy-start = (f32[8,1]{1,0:T(8,128)S(1)}, f32[8,1]{1,0:T(8,128)}, u32[]{:S(2)}) copy-start(f32[8,1]{1,0:T(8,128)} %get-tuple-element.8) | copy-start | bytes 100
  81.1 1.3 %copy-start.2 = (f32[8,64]{1,0:T(8,128)S(1)}, f32[8,64]{1,0:T(8,128)}, u32[]{:S(2)}) copy-start(f32[8,64]{1,0:T(8,128)} %get-tuple-element.12) | copy-start | bytes 6148

commit v3 on v2

--- a/solution.py
+++ b/solution.py
@@ -44,7 +44,8 @@
     s_x1, r_x1, s_w, r_w, s_x2, r_up, r_dn, s_x3, r_x3, s_p, r_p, s_f, r_f,
 ):
     traces, toks, _ = hid.shape
-    half = traces // 2
+    half = traces
+    block = bnd.shape[1] // 2
     planes = n_seq // 2
     depth = w.shape[0]
     cols = w.shape[1] // 2
@@ -64,6 +65,23 @@
     h_core = h + 1 - 2 * (h % 2)
     h_x = lax.rem(h + 2, n_head)
 
+    barrier = pltpu.get_barrier_semaphore()
+
+    def greet(to_s, to_h):
+        pl.semaphore_signal(barrier, inc=1, device_id=(to_s, to_h), device_id_type=MESH)
+
+    greet(across, h)
+    greet(s, h_core)
+    greet(s, h_x)
+
+    @pl.when(z > 0)
+    def _():
+        greet(s - 2, h)
+
+    @pl.when(z < planes - 1)
+    def _():
+        greet(s + 2, h)
+
     def pick(t):
         pos = lax.broadcasted_iota(jnp.int32, (toks, bnd.shape[1]), 0) + s * toks
         hot = jnp.where(bnd[pl.ds(t, 1), :] == pos, 1.0, 0.0).astype(jnp.bfloat16)
@@ -84,16 +102,24 @@
         rows = pl.ds(pl.multiple_of(y * depth + i * part, part), part)
         return remote(wown.at[pl.ds(i * part, part)], wall.at[rows], s_w.at[i], r_w.at[i], across, h)
 
+    def pick_half(which, dst):
+        for i in range(traces // 2):
+            got = pick(which * (traces // 2) + i)
+            dst[2 * i] = got[:block]
+            dst[2 * i + 1] = got[block:]
+
+    pick_half(other, xout)
     wown[...] = w[:, my_cols(other)]
-    copy_w(0).start()
+    pl.semaphore_wait(
+        barrier, 3 + jnp.where(z > 0, 1, 0) + jnp.where(z < planes - 1, 1, 0)
+    )
     for k in range(half):
-        xout[k] = pick(other * half + k)
         copy_x1(k).start()
-    copy_w(1).start()
+    for i in range(2):
+        copy_w(i).start()
     wall[pl.ds(pl.multiple_of(y * depth, depth), depth), :] = w[:, my_cols(y)]
 
-    for k in range(half):
-        xacc[k] = pick(y * half + k)
+    pick_half(y, xacc)
 
     same_core = (h % 2) == (z % 2)
 
@@ -163,23 +189,16 @@
 
     for k in range(half):
         chain(k)
-    for k in range(half):
-        spread(k)
-    for k in range(half):
-        spread_far(k)
-    for i in range(2):
-        copy_w(i).wait_recv()
-
     def copy_p(t, down):
         to_s = lax.rem(s + n_seq - 2, n_seq) if down else lax.rem(s + 2, n_seq)
         return remote(psend.at[t], precv.at[t], s_p.at[t], r_p.at[t], to_s, h)
 
     bias = b[:, my_cols(y)]
     out_row = w2[:, my_cols(y)]
-    lanes = lax.broadcasted_iota(jnp.int32, (xall.shape[1], 128), 1)
+    lanes = lax.broadcasted_iota(jnp.int32, (block, 128), 1)
     fsend[...] = jnp.zeros_like(fsend)
 
-    def reduce_step(tick, _):
+    def reduce_step(tick):
         for down in (True, False):
             first = planes - 1 if down else 0
             last = planes - 1 - first
@@ -203,11 +222,18 @@
                 def _():
                     act = jnp.maximum(psend[t] + bias, 0.0) * out_row
                     total = jnp.sum(act, axis=1, keepdims=True)
-                    fsend[...] = fsend[...] + jnp.where(lanes == t, total, 0.0)
-
-        return 0
-
-    lax.fori_loop(0, half + planes - 1, reduce_step, 0)
+                    here = pl.ds(pl.multiple_of((k % 2) * block, block), block)
+                    fsend[here, :] = fsend[here, :] + jnp.where(lanes == t // 2, total, 0.0)
+
+    for k in range(half):
+        spread(k)
+        spread_far(k)
+        if k == 0:
+            for i in range(2):
+                copy_w(i).wait_recv()
+        reduce_step(k)
+    for k in range(half, half + planes - 1):
+        reduce_step(k)
 
     is_end = (z == 0) | (z == planes - 1)
     slots = 4 * n_head
@@ -288,7 +314,7 @@
     traces, toks, feats = hidden_states.shape
     steps = boundary.shape[1]
     depth, width = w_first.shape
-    half, cols = traces // 2, width // 2
+    half, block, cols = traces, steps // 2, width // 2
     bf16, f32 = jnp.bfloat16, jnp.float32
     dma = pltpu.SemaphoreType.DMA
     vmem = pl.BlockSpec(memory_space=pltpu.VMEM)
@@ -302,26 +328,26 @@
         in_specs=[vmem] * 7,
         out_specs=(vmem,) * 3,
         scratch_shapes=[
-            pltpu.VMEM((half, steps, feats), bf16),
-            pltpu.VMEM((half, steps, feats), bf16),
-            pltpu.VMEM((half, steps, feats), bf16),
-            pltpu.VMEM((half, steps, feats), bf16),
-            pltpu.VMEM((half, steps, feats), bf16),
-            pltpu.VMEM((traces, steps, feats), bf16),
+            pltpu.VMEM((half, block, feats), bf16),
+            pltpu.VMEM((half, block, feats), bf16),
+            pltpu.VMEM((half, block, feats), bf16),
+            pltpu.VMEM((half, block, feats), bf16),
+            pltpu.VMEM((half, block, feats), bf16),
+            pltpu.VMEM((2 * half, block, feats), bf16),
             pltpu.VMEM((depth, cols), bf16),
             pltpu.VMEM((2 * depth, cols), bf16),
-            pltpu.VMEM((traces, steps, cols), f32),
-            pltpu.VMEM((traces, steps, cols), f32),
+            pltpu.VMEM((2 * half, block, cols), f32),
+            pltpu.VMEM((2 * half, block, cols), f32),
             pltpu.VMEM((steps, 128), f32),
             pltpu.VMEM((4 * n_head, traces, steps), f32),
             dma((half,)), dma((half,)),
             dma((2,)), dma((2,)),
             dma((half,)), dma((half,)), dma((half,)),
-            dma((traces, 3)), dma((traces,)),
-            dma((traces,)), dma((traces,)),
+            dma((2 * half, 3)), dma((2 * half,)),
+            dma((2 * half,)), dma((2 * half,)),
             dma((n_seq * n_head,)), dma((4 * n_head,)),
         ],
-        compiler_params=pltpu.CompilerParams(has_side_effects=True),
+        compiler_params=pltpu.CompilerParams(collective_id=0, has_side_effects=True),
     )(
         hidden_states, boundary, valid, pairs, w_first,
         b_first.reshape(1, width), w_second.reshape(1, width),

time: 83.2 us -> 77.7 us (0.934)
  Pallas kernels: 78.5 us -> 73 us
    pallas_call x1, Pallas kernels: 78.5 us -> 73 us  [fused(): pl.pallas_call(functools.partial(kernel, n_seq, n_head), out_shape=(jax.S...]
where the time goes in v3:
time: 77.7 us; the launch traced here: 77.5 us
  Pallas kernels  73 us (94%)
  local copies, waits for them, and re-layouts  2.6 us (3%)
  other arithmetic  1.25 us (2%)
    pallas_call x1, Pallas kernels, fused(): pl.pallas_call(functools.partial(kernel, n_seq, n_head), out_shape=(jax.S...  73 us
    unnamed x10, local copies, waits for them, and re-layouts  2.6 us

profile of v3, /device:TPU:0, one launch (start us, length us, event | category | flops | bytes accessed | tf_op | source)
XLA Modules:
  0.0 77.5 jit_solution(2349290016311949987)
XLA Ops:
  0.6 0.0 copy-start.3
  0.6 0.7 copy-done.3
  1.3 0.7 copy.11.pairs
  2.0 73.0 %shard_map.94 = (f32[8,64]{1,0:T(8,128)}, f32[8,1]{1,0:T(8,128)}, f32[8,1]{1,0:T(8,128)}) custom-call(bf16[8,64,896]{2,1,0:T(8,128)(2,1)} %hid.1, s32[8,64]{1,0:T(8,128)} %bnd.1, s32[8,64]{1,0:T(8,128)} %valid.1, s32[8,2]{1,0:T(8,128)} %copy.11.pairs, bf16[448,1024]{1,0:T(8,128)(2,1)} %w.1, f32[1,1024]{1,0:T(1,128)} %bitcast.2, f32[1,1024]{1,0:T(1,128)} %bitcast.3), custom_call_target="tpu_custom_call" | custom-call | tf_op jit(solution)/shard_map/pallas_call | solution.py:321
  75.0 0.0 copy-start.1
  75.0 0.0 copy-start
  75.0 0.7 copy-done.1
  75.7 0.0 copy-start.2
  75.7 0.6 reduce
  76.3 0.0 copy-done
  76.3 0.6 reduce.1
  76.9 0.0 copy-done.2
  76.9 0.6 copy.13
Async XLA Ops:
  0.6 0.7 copy-start.3
  75.0 0.7 copy-start.1
  75.0 1.3 %copy-start = (f32[8,1]{1,0:T(8,128)S(1)}, f32[8,1]{1,0:T(8,128)}, u32[]{:S(2)}) copy-start(f32[8,1]{1,0:T(8,128)} %get-tuple-element.8) | copy-start | bytes 100
  75.7 1.3 %copy-start.2 = (f32[8,64]{1,0:T(8,128)S(1)}, f32[8,64]{1,0:T(8,128)}, u32[]{:S(2)}) copy-start(f32[8,64]{1,0:T(8,128)} %get-tuple-element.12) | copy-start | bytes 6148

commit v4 on v3

--- a/solution.py
+++ b/solution.py
@@ -39,10 +39,15 @@
 
 
 def kernel(
-    n_seq, n_head, hid, bnd, valid, pairs, w, b, w2, reward, score, margin,
+    n_seq, n_head, hid_hbm, bnd, valid, pairs, w_hbm, b, w2, reward, score, margin,
+    hid, w, s_hid, s_win,
     xout, xin, xacc, xup, xdn, xall, wown, wall, psend, precv, fsend, frecv,
     s_x1, r_x1, s_w, r_w, s_x2, r_up, r_dn, s_x3, r_x3, s_p, r_p, s_f, r_f,
 ):
+    fetch_hid = pltpu.make_async_copy(hid_hbm, hid, s_hid)
+    fetch_w = pltpu.make_async_copy(w_hbm, w, s_win)
+    fetch_hid.start()
+    fetch_w.start()
     traces, toks, _ = hid.shape
     half = traces
     block = bnd.shape[1] // 2
@@ -108,13 +113,15 @@
             dst[2 * i] = got[:block]
             dst[2 * i + 1] = got[block:]
 
+    fetch_hid.wait()
     pick_half(other, xout)
-    wown[...] = w[:, my_cols(other)]
     pl.semaphore_wait(
         barrier, 3 + jnp.where(z > 0, 1, 0) + jnp.where(z < planes - 1, 1, 0)
     )
     for k in range(half):
         copy_x1(k).start()
+    fetch_w.wait()
+    wown[...] = w[:, my_cols(other)]
     for i in range(2):
         copy_w(i).start()
     wall[pl.ds(pl.multiple_of(y * depth, depth), depth), :] = w[:, my_cols(y)]
@@ -227,6 +234,7 @@
 
     for k in range(half):
         spread(k)
+    for k in range(half):
         spread_far(k)
         if k == 0:
             for i in range(2):
@@ -265,14 +273,12 @@
     live = valid[...] == 1
     reward[...] = jnp.where(live, logit, 0.0)
     low = jnp.min(jnp.where(live, logit, 1e30), axis=1, keepdims=True)
-    score[...] = low
-    eye = lax.broadcasted_iota(jnp.int32, (traces, traces), 0) == lax.broadcasted_iota(
-        jnp.int32, (traces, traces), 1
-    )
-    row = jnp.sum(jnp.where(eye, low, 0.0), axis=0, keepdims=True)
-    ids = lax.broadcasted_iota(jnp.int32, (pairs.shape[0], traces), 1)
-    winner = jnp.sum(jnp.where(pairs[:, 0:1] == ids, row, 0.0), axis=1, keepdims=True)
-    loser = jnp.sum(jnp.where(pairs[:, 1:2] == ids, row, 0.0), axis=1, keepdims=True)
+    square = (traces, traces)
+    eye = lax.broadcasted_iota(jnp.int32, square, 0) == lax.broadcasted_iota(jnp.int32, square, 1)
+    score[...] = jnp.sum(jnp.where(eye, low, 0.0), axis=0)
+    ids = lax.broadcasted_iota(jnp.int32, (traces, pairs.shape[1]), 0)
+    winner = jnp.sum(jnp.where(pairs[0:1, :] == ids, low, 0.0), axis=0)
+    loser = jnp.sum(jnp.where(pairs[1:2, :] == ids, low, 0.0), axis=0)
     margin[...] = winner - loser
 
     for i in range(2):
@@ -318,16 +324,20 @@
     bf16, f32 = jnp.bfloat16, jnp.float32
     dma = pltpu.SemaphoreType.DMA
     vmem = pl.BlockSpec(memory_space=pltpu.VMEM)
-    reward, score, margin = pl.pallas_call(
+    hbm = pl.BlockSpec(memory_space=pl.ANY)
+    return pl.pallas_call(
         functools.partial(kernel, n_seq, n_head),
         out_shape=(
             jax.ShapeDtypeStruct((traces, steps), f32),
-            jax.ShapeDtypeStruct((traces, 1), f32),
-            jax.ShapeDtypeStruct((pairs.shape[0], 1), f32),
+            jax.ShapeDtypeStruct((traces,), f32),
+            jax.ShapeDtypeStruct((pairs.shape[0],), f32),
         ),
-        in_specs=[vmem] * 7,
+        in_specs=[hbm] + [vmem] * 3 + [hbm] + [vmem] * 2,
         out_specs=(vmem,) * 3,
         scratch_shapes=[
+            pltpu.VMEM((traces, toks, feats), bf16),
+            pltpu.VMEM((depth, width), bf16),
+            dma, dma,
             pltpu.VMEM((half, block, feats), bf16),
             pltpu.VMEM((half, block, feats), bf16),
             pltpu.VMEM((half, block, feats), bf16),
@@ -349,10 +359,9 @@
         ],
         compiler_params=pltpu.CompilerParams(collective_id=0, has_side_effects=True),
     )(
-        hidden_states, boundary, valid, pairs, w_first,
+        hidden_states, boundary, valid, pairs.T, w_first,
         b_first.reshape(1, width), w_second.reshape(1, width),
     )
-    return reward, score.reshape(traces), margin.reshape(pairs.shape[0])
 
 
 def solution(mesh):

time: 77.7 us -> 72.8 us (0.937)
  Pallas kernels: 73 us -> 69.5 us
  other arithmetic: 1.25 us -> 0 us
    pallas_call x1, Pallas kernels: 73 us -> 69.5 us  [fused(): pl.pallas_call(functools.partial(kernel, n_seq, n_head), out_shape=(jax.S...]
    pallas_call x2 -> x0, other arithmetic: 1.25 us -> none  [fused(): pl.pallas_call(functools.partial(kernel, n_seq, n_head), out_shape=(jax.S...]
    unnamed x10 -> x9, local copies, waits for them, and re-layouts: 2.6 us -> 2.38 us
where the time goes in v4:
time: 72.8 us; the launch traced here: 72.5 us
  Pallas kernels  69.5 us (95%)
  local copies, waits for them, and re-layouts  2.38 us (3%)
    pallas_call x1, Pallas kernels, fused(): pl.pallas_call(functools.partial(kernel, n_seq, n_head), out_shape=(jax.S...  69.5 us
    unnamed x9, local copies, waits for them, and re-layouts  2.38 us

profile of v4, /device:TPU:0, one launch (start us, length us, event | category | flops | bytes accessed | tf_op | source)
XLA Modules:
  0.0 72.5 jit_solution(4333334990384855211)
XLA Ops:
  0.6 69.5 %shard_map.94 = (f32[8,64]{1,0:T(8,128)}, f32[8]{0:T(128)}, f32[8]{0:T(128)}) custom-call(bf16[8,64,896]{2,1,0:T(8,128)(2,1)} %hid_hbm.1, s32[8,64]{1,0:T(8,128)} %bnd.1, s32[8,64]{1,0:T(8,128)} %valid.1, s32[2,8]{1,0:T(2,128)} %bitcast.5, bf16[448,1024]{1,0:T(8,128)(2,1)} %w_hbm.1, f32[1,1024]{1,0:T(1,128)} %bitcast.3, f32[1,1024]{1,0:T(1,128)} %bitcast.4), custom_call_target="tpu_custom_call" | custom-call | tf_op jit(solution)/shard_map/pallas_call | solution.py:328
  70.1 0.0 copy-start
  70.2 0.7 copy-done
  70.8 0.0 copy-start.2
  70.8 0.6 copy.13
  71.4 0.0 copy-done.2
  71.4 0.0 copy-start.1
  71.4 0.5 copy.14
  71.9 0.1 copy-done.1
  72.0 0.5 copy.15
Async XLA Ops:
  70.1 0.7 copy-start
  70.8 0.6 copy-start.2
  71.4 0.6 copy-start.1

commit v5 on v4

--- a/solution.py
+++ b/solution.py
@@ -205,11 +205,13 @@
     lanes = lax.broadcasted_iota(jnp.int32, (block, 128), 1)
     fsend[...] = jnp.zeros_like(fsend)
 
+    lag = 3
+
     def reduce_step(tick):
         for down in (True, False):
             first = planes - 1 if down else 0
             last = planes - 1 - first
-            k = tick - (planes - 1 - z if down else z)
+            k = tick - lag * (planes - 1 - z if down else z)
             t = k if down else half + k
 
             @pl.when((k >= 0) & (k < half))
@@ -240,7 +242,7 @@
             for i in range(2):
                 copy_w(i).wait_recv()
         reduce_step(k)
-    for k in range(half, half + planes - 1):
+    for k in range(half, half + lag * (planes - 1)):
         reduce_step(k)
 
     is_end = (z == 0) | (z == planes - 1)

time: 72.8 us -> 62.4 us (0.86)
  Pallas kernels: 69.5 us -> 59.1 us
    pallas_call x1, Pallas kernels: 69.5 us -> 59.1 us  [fused(): pl.pallas_call(functools.partial(kernel, n_seq, n_head), out_shape=(jax.S...]
where the time goes in v5:
time: 62.4 us; the launch traced here: 62.1 us
  Pallas kernels  59.1 us (95%)
  local copies, waits for them, and re-layouts  2.38 us (4%)
  between operations  0.65 us (1%)
    pallas_call x1, Pallas kernels, fused(): pl.pallas_call(functools.partial(kernel, n_seq, n_head), out_shape=(jax.S...  59.1 us
    unnamed x9, local copies, waits for them, and re-layouts  2.38 us

profile of v5, /device:TPU:0, one launch (start us, length us, event | category | flops | bytes accessed | tf_op | source)
XLA Modules:
  0.0 62.1 jit_solution(509255065657196389)
XLA Ops:
  0.6 59.1 %shard_map.94 = (f32[8,64]{1,0:T(8,128)}, f32[8]{0:T(128)}, f32[8]{0:T(128)}) custom-call(bf16[8,64,896]{2,1,0:T(8,128)(2,1)} %hid_hbm.1, s32[8,64]{1,0:T(8,128)} %bnd.1, s32[8,64]{1,0:T(8,128)} %valid.1, s32[2,8]{1,0:T(2,128)} %bitcast.5, bf16[448,1024]{1,0:T(8,128)(2,1)} %w_hbm.1, f32[1,1024]{1,0:T(1,128)} %bitcast.3, f32[1,1024]{1,0:T(1,128)} %bitcast.4), custom_call_target="tpu_custom_call" | custom-call | tf_op jit(solution)/shard_map/pallas_call | solution.py:330
  59.7 0.0 copy-start
  59.7 0.7 %copy-done = f32[8,64]{1,0:T(8,128)S(1)} copy-done((f32[8,64]{1,0:T(8,128)S(1)}, f32[8,64]{1,0:T(8,128)}, u32[]{:S(2)}) %copy-start) | copy-done | bytes 2072
  60.4 0.0 copy-start.2
  60.4 0.6 copy.13
  61.0 0.0 copy-done.2
  61.0 0.0 copy-start.1
  61.0 0.5 copy.14
  61.5 0.1 copy-done.1
  61.6 0.5 copy.15
Async XLA Ops:
  59.7 0.7 %copy-start = (f32[8,64]{1,0:T(8,128)S(1)}, f32[8,64]{1,0:T(8,128)}, u32[]{:S(2)}) copy-start(f32[8,64]{1,0:T(8,128)} %get-tuple-element.6) | copy-start | bytes 6148
  60.4 0.6 copy-start.2
  61.0 0.6 copy-start.1

commit v6 on v5

--- a/solution.py
+++ b/solution.py
@@ -232,7 +232,7 @@
                     act = jnp.maximum(psend[t] + bias, 0.0) * out_row
                     total = jnp.sum(act, axis=1, keepdims=True)
                     here = pl.ds(pl.multiple_of((k % 2) * block, block), block)
-                    fsend[here, :] = fsend[here, :] + jnp.where(lanes == t // 2, total, 0.0)
+                    fsend[here, :] = fsend[here, :] + jnp.where(lanes == k // 2, total, 0.0)
 
     for k in range(half):
         spread(k)
@@ -263,14 +263,17 @@
         for d in range(1, n_dev):
             copy_f(d).start()
 
-    logit = jnp.zeros(frecv.shape[1:], jnp.float32)
+    sums = [jnp.zeros(frecv.shape[1:], jnp.float32) for _ in range(2)]
     for i in range(slots):
 
         @pl.when(jnp.logical_not(is_end & (slot == i)))
         def _():
             remote(frecv.at[i], frecv.at[i], s_f.at[0], r_f.at[i], across, h).wait_recv()
 
-        logit = logit + frecv[i]
+        side = i // (2 * n_head)
+        sums[side] = sums[side] + frecv[i]
+
+    logit = jnp.concatenate(sums, axis=0)
 
     live = valid[...] == 1
     reward[...] = jnp.where(live, logit, 0.0)
@@ -351,7 +354,7 @@
             pltpu.VMEM((2 * half, block, cols), f32),
             pltpu.VMEM((2 * half, block, cols), f32),
             pltpu.VMEM((steps, 128), f32),
-            pltpu.VMEM((4 * n_head, traces, steps), f32),
+            pltpu.VMEM((4 * n_head, traces // 2, steps), f32),
             dma((half,)), dma((half,)),
             dma((2,)), dma((2,)),
             dma((half,)), dma((half,)), dma((half,)),

time: 62.4 us -> 62.4 us (level)
  no operation moved by 1% of the time
where the time goes in v6:
time: 62.4 us; the launch traced here: 62.1 us
  Pallas kernels  59.1 us (95%)
  local copies, waits for them, and re-layouts  2.38 us (4%)
  between operations  0.65 us (1%)
    pallas_call x1, Pallas kernels, fused(): pl.pallas_call(functools.partial(kernel, n_seq, n_head), out_shape=(jax.S...  59.1 us
    unnamed x9, local copies, waits for them, and re-layouts  2.38 us

profile of v6, /device:TPU:0, one launch (start us, length us, event | category | flops | bytes accessed | tf_op | source)
XLA Modules:
  0.0 62.1 jit_solution(18309410453814387260)
XLA Ops:
  0.6 59.1 %shard_map.94 = (f32[8,64]{1,0:T(8,128)}, f32[8]{0:T(128)}, f32[8]{0:T(128)}) custom-call(bf16[8,64,896]{2,1,0:T(8,128)(2,1)} %hid_hbm.1, s32[8,64]{1,0:T(8,128)} %bnd.1, s32[8,64]{1,0:T(8,128)} %valid.1, s32[2,8]{1,0:T(2,128)} %bitcast.5, bf16[448,1024]{1,0:T(8,128)(2,1)} %w_hbm.1, f32[1,1024]{1,0:T(1,128)} %bitcast.3, f32[1,1024]{1,0:T(1,128)} %bitcast.4), custom_call_target="tpu_custom_call" | custom-call | tf_op jit(solution)/shard_map/pallas_call | solution.py:333
  59.7 0.0 copy-start
  59.7 0.7 %copy-done = f32[8,64]{1,0:T(8,128)S(1)} copy-done((f32[8,64]{1,0:T(8,128)S(1)}, f32[8,64]{1,0:T(8,128)}, u32[]{:S(2)}) %copy-start) | copy-done | bytes 2072
  60.4 0.0 copy-start.2
  60.4 0.6 copy.13
  61.0 0.0 copy-done.2
  61.0 0.0 copy-start.1
  61.0 0.5 copy.14
  61.5 0.1 copy-done.1
  61.6 0.5 copy.15
Async XLA Ops:
  59.7 0.7 %copy-start = (f32[8,64]{1,0:T(8,128)S(1)}, f32[8,64]{1,0:T(8,128)}, u32[]{:S(2)}) copy-start(f32[8,64]{1,0:T(8,128)} %get-tuple-element.6) | copy-start | bytes 6148
  60.4 0.6 copy-start.2
  61.0 0.6 copy-start.1

commit v7 on v6

--- a/solution.py
+++ b/solution.py
@@ -107,26 +107,27 @@
         rows = pl.ds(pl.multiple_of(y * depth + i * part, part), part)
         return remote(wown.at[pl.ds(i * part, part)], wall.at[rows], s_w.at[i], r_w.at[i], across, h)
 
-    def pick_half(which, dst):
+    def pick_half(which, dst, send):
         for i in range(traces // 2):
             got = pick(which * (traces // 2) + i)
             dst[2 * i] = got[:block]
             dst[2 * i + 1] = got[block:]
+            if send:
+                copy_x1(2 * i).start()
+                copy_x1(2 * i + 1).start()
 
     fetch_hid.wait()
-    pick_half(other, xout)
     pl.semaphore_wait(
         barrier, 3 + jnp.where(z > 0, 1, 0) + jnp.where(z < planes - 1, 1, 0)
     )
-    for k in range(half):
-        copy_x1(k).start()
+    pick_half(other, xout, True)
     fetch_w.wait()
     wown[...] = w[:, my_cols(other)]
     for i in range(2):
         copy_w(i).start()
     wall[pl.ds(pl.multiple_of(y * depth, depth), depth), :] = w[:, my_cols(y)]
 
-    pick_half(y, xacc)
+    pick_half(y, xacc, False)
 
     same_core = (h % 2) == (z % 2)
 

time: 62.4 us -> 62.6 us (level)
  no operation moved by 1% of the time
where the time goes in v7:
time: 62.6 us; the launch traced here: 62.3 us
  Pallas kernels  59.3 us (95%)
  local copies, waits for them, and re-layouts  2.38 us (4%)
  between operations  0.65 us (1%)
    pallas_call x1, Pallas kernels, fused(): pl.pallas_call(functools.partial(kernel, n_seq, n_head), out_shape=(jax.S...  59.3 us
    unnamed x9, local copies, waits for them, and re-layouts  2.38 us

profile of v7, /device:TPU:0, one launch (start us, length us, event | category | flops | bytes accessed | tf_op | source)
XLA Modules:
  0.0 62.3 jit_solution(11433518511012149873)
XLA Ops:
  0.6 59.3 %shard_map.94 = (f32[8,64]{1,0:T(8,128)}, f32[8]{0:T(128)}, f32[8]{0:T(128)}) custom-call(bf16[8,64,896]{2,1,0:T(8,128)(2,1)} %hid_hbm.1, s32[8,64]{1,0:T(8,128)} %bnd.1, s32[8,64]{1,0:T(8,128)} %valid.1, s32[2,8]{1,0:T(2,128)} %bitcast.5, bf16[448,1024]{1,0:T(8,128)(2,1)} %w_hbm.1, f32[1,1024]{1,0:T(1,128)} %bitcast.3, f32[1,1024]{1,0:T(1,128)} %bitcast.4), custom_call_target="tpu_custom_call" | custom-call | tf_op jit(solution)/shard_map/pallas_call | solution.py:334
  59.9 0.0 copy-start
  59.9 0.7 %copy-done = f32[8,64]{1,0:T(8,128)S(1)} copy-done((f32[8,64]{1,0:T(8,128)S(1)}, f32[8,64]{1,0:T(8,128)}, u32[]{:S(2)}) %copy-start) | copy-done | bytes 2072
  60.6 0.0 copy-start.2
  60.6 0.6 copy.13
  61.2 0.0 copy-done.2
  61.2 0.0 copy-start.1
  61.2 0.5 copy.14
  61.7 0.1 copy-done.1
  61.8 0.5 copy.15
Async XLA Ops:
  59.9 0.7 %copy-start = (f32[8,64]{1,0:T(8,128)S(1)}, f32[8,64]{1,0:T(8,128)}, u32[]{:S(2)}) copy-start(f32[8,64]{1,0:T(8,128)} %get-tuple-element.6) | copy-start | bytes 6148
  60.6 0.6 copy-start.2
  61.2 0.6 copy-start.1
